TPU v7x, 32 devices: a whole 2x2x4 slice. The times are simulated.
32 devices in a mesh: row: 8 (over z, x), col: 4 (over y, core).
Axes of the slice: x: 2, y: 2, z: 4, core: 2. Of those that a mesh axis runs over, the one named last changes fastest.
Arguments:
- frontier: bfloat16 [8192, 128], P(('row', 'col')), may hold values from 0 to 8, as said below
- visited: int32 [8192, 128], P(('row', 'col')), may hold values 0 or 1
- tile_rows: int32 [8, 4, 8, 20], P('row', 'col'), may hold values from 0 to 1
- tile_cols: int32 [8, 4, 8, 20], P('row', 'col'), may hold values from 0 to 7
- tile_bits: bfloat16 [8, 4, 8, 20, 128, 128], P('row', 'col'), may hold values from 0 to 1, as said below
Outputs:
- depth_out: int32 [8192, 128], P(('row', 'col'))
- reach_out: float32 [8192, 128], P(('row', 'col'))
Inputs may be any that keep to these rules, and one draw needn't show every extreme that they name: `frontier`: every entry is 0 or lies between 0.25 and 8. `tile_bits`: entries are 0 or 1.
All inputs are finite; a program needn't handle non-finite values. No bound on the sum of `visited` on one device may be relied on, other than what follows from the above.
Results may differ from a plain program's by a relative error of at most 0.0065.
Values may be sent and summed in bfloat16 or wider, within the bound.
A program may use at most 64 MiB of HBM per device.

v0:
```python
import jax
import jax.numpy as jnp
from jax import lax
from jax.sharding import PartitionSpec as P

LEVELS = 4


def on_device(frontier, visited, tile_rows, tile_cols, tile_bits):
    row_index = tile_rows[0, 0]
    col_index = tile_cols[0, 0]
    tile_data = tile_bits[0, 0]
    per_dev, sources = frontier.shape
    tile_size = tile_data.shape[-1]
    col_tiles = lax.axis_size("col") * per_dev // tile_size
    col_onehot = (
        col_index[:, :, None] == jnp.arange(col_tiles, dtype=jnp.int32)[None, None, :]
    ).astype(jnp.float32)
    visited_now = (visited != 0) | (frontier > 0)
    depth_out = jnp.where(visited_now, 0, LEVELS + 1).astype(jnp.int32)
    reach_out = frontier.astype(jnp.float32)
    scaling = jnp.ones((sources,), jnp.float32)
    current = frontier
    for level_step in range(1, LEVELS + 1):
        gathered = lax.all_gather(current, "row", axis=0, tiled=True)
        shard_count = gathered.shape[0] // per_dev
        blocked = gathered.reshape(shard_count, per_dev // tile_size, tile_size, sources)
        picked = jnp.take_along_axis(blocked, row_index[:, :, None, None], axis=1)
        products = jnp.einsum(
            "qtkn,qtks->qtns", tile_data, picked, preferred_element_type=jnp.float32
        )
        partial_value = jnp.einsum(
            "qtm,qtns->mns",
            col_onehot,
            products,
            precision=lax.Precision.HIGHEST,
            preferred_element_type=jnp.float32,
        )
        raw_sum = lax.psum_scatter(
            partial_value.reshape(-1, sources).astype(jnp.bfloat16),
            "col",
            scatter_dimension=0,
            tiled=True,
        ).astype(jnp.float32)
        newly_hit = (raw_sum > 0) & jnp.logical_not(visited_now)
        reached = jnp.where(newly_hit, raw_sum, jnp.zeros_like(raw_sum))
        counted = jnp.sum(newly_hit.astype(jnp.float32), axis=0)
        totals = jnp.sum(reached, axis=0)
        counted, totals = lax.psum((counted, totals), ("row", "col"))
        scaling = scaling / jnp.maximum(scaling * totals / jnp.maximum(counted, 1.0), 1.0)
        reach_out = reach_out + scaling[None, :] * reached
        depth_out = jnp.where(newly_hit, level_step, depth_out)
        visited_now = visited_now | newly_hit
        current = reached.astype(jnp.bfloat16)
    return (depth_out, reach_out)


def solution(mesh):
    placed = (
        P(("row", "col"), None),
        P(("row", "col"), None),
        P("row", "col", None, None),
        P("row", "col", None, None),
        P("row", "col", None, None, None, None),
    )
    return jax.shard_map(
        on_device,
        mesh=mesh,
        in_specs=placed,
        out_specs=(P(("row", "col"), None), P(("row", "col"), None)),
        check_vma=False,
    )
```

profile of v0, /device:TPU:0, one launch (start us, length us, event | category | flops | bytes accessed | tf_op | source)
XLA Modules:
  0.0 445.9 jit_solution(860876956006624836)
XLA Ops:
  8.7 33.2 %all_gather.12 = bf16[2048,128]{1,0:T(8,128)(2,1)S(1)} all-gather(bf16[256,128]{1,0:T(8,128)(2,1)} %param.7), channel_id=1, replica_groups=mesh['row'=8,'col'=4] {'row'}, dimensions={0}, use_global_device_ids=true | all-gather | bytes 589824 | tf_op jit(solution)/shard_map/all_gather | solution.py:25
  41.9 12.2 %gather_fusion = bf16[160,128,128]{2,1,0:T(8,128)(2,1)} fusion(bf16[8,2,128,128]{3,2,1,0:T(8,128)(2,1)S(1)} %bitcast.97, s32[160]{0:T(256)S(1)} %reshape.99), kind=kCustom, calls=%fused_computation.clone | custom fusion | bytes 10487040 | tf_op jit(solution)/shard_map/jit(take_along_axis)/gather | solution.py:28
  54.1 10.0 %fusion.14 = f32[8,20,128,128]{3,2,1,0:T(8,128)} fusion(bf16[1,1,8,20,128,128]{5,4,3,2,1,0:T(8,128)(2,1)} %param.11, bf16[8,20,128,128]{3,2,1,0:T(8,128)(2,1)} %bitcast.99, pred[8,20]{1,0:T(8,128)(4,1)S(1)} %and_bitcast_fusion), kind=kOutput, calls=%fused_computation.18 | convolution fusion | flops 673710080 | bytes 20971680 | tf_op jit(solution)/shard_map/qtkn,qtks->qtns/dot_general | solution.py:29
  64.1 11.9 %copy.11 = f32[8,20,128,128]{2,1,0,3:T(8,128)} copy(f32[8,20,128,128]{3,2,1,0:T(8,128)} %fusion.14) | data formatting | bytes 20971520 | tf_op jit(solution)/shard_map/qtkn,qtks->qtns/dot_general | solution.py:29
  76.0 8.2 %fusion.49 = bf16[8,128,128]{2,0,1:T(8,128)(2,1)S(1)} fusion(f32[8,20,128,128]{2,1,0,3:T(8,128)} %copy.11, s32[8,20]{1,0:T(8,128)S(1)} %bitcast.106), kind=kOutput, calls=%fused_computation.39 | convolution fusion | flops 251790592 | bytes 10748544 | tf_op jit(solution)/shard_map/qtm,qtns->mns/dot_general | solution.py:32
  85.0 21.2 %reduce-scatter.5.cloned.1.call-done = bf16[256,128]{1,0:T(8,128)(2,1)} async-done(((bf16[1024,128]{1,0:T(8,128)(2,1)}), bf16[256,128]{1,0:T(8,128)(2,1)}) %reduce-scatter.5.cloned.1.call-update) | async-done | bytes 65552 | tf_op jit(solution)/shard_map/reduce_scatter | solution.py:39
  108.0 32.1 %all_gather.13 = bf16[2048,128]{1,0:T(8,128)(2,1)S(1)} all-gather(bf16[256,128]{1,0:T(8,128)(2,1)S(1)} %fusion.54), channel_id=1, replica_groups=mesh['row'=8,'col'=4] {'row'}, dimensions={0}, use_global_device_ids=true | all-gather | bytes 589824 | tf_op jit(solution)/shard_map/all_gather | solution.py:25
  140.1 12.2 %gather_fusion.1 = bf16[160,128,128]{2,1,0:T(8,128)(2,1)} fusion(bf16[8,2,128,128]{3,2,1,0:T(8,128)(2,1)S(1)} %bitcast.95, s32[160]{0:T(256)S(1)} %reshape.99), kind=kCustom, calls=%fused_computation.1.clone | custom fusion | bytes 10487040 | tf_op jit(solution)/shard_map/jit(take_along_axis)/gather | solution.py:28
  152.3 10.0 %fusion.12 = f32[8,20,128,128]{3,2,1,0:T(8,128)} fusion(bf16[1,1,8,20,128,128]{5,4,3,2,1,0:T(8,128)(2,1)} %param.11, bf16[8,20,128,128]{3,2,1,0:T(8,128)(2,1)} %bitcast.100, pred[8,20]{1,0:T(8,128)(4,1)S(1)} %and_bitcast_fusion), kind=kOutput, calls=%fused_computation.16 | convolution fusion | flops 673710080 | bytes 20971680 | tf_op jit(solution)/shard_map/qtkn,qtks->qtns/dot_general | solution.py:29
  162.3 11.9 %copy.13 = f32[8,20,128,128]{2,1,0,3:T(8,128)} copy(f32[8,20,128,128]{3,2,1,0:T(8,128)} %fusion.12) | data formatting | bytes 20971520 | tf_op jit(solution)/shard_map/qtkn,qtks->qtns/dot_general | solution.py:29
  174.2 8.1 %fusion.46 = bf16[8,128,128]{2,0,1:T(8,128)(2,1)S(1)} fusion(f32[8,20,128,128]{2,1,0,3:T(8,128)} %copy.13, s32[8,20]{1,0:T(8,128)S(1)} %bitcast.107), kind=kOutput, calls=%fused_computation.38 | convolution fusion | flops 251790592 | bytes 10748544 | tf_op jit(solution)/shard_map/qtm,qtns->mns/dot_general | solution.py:32
  183.1 20.1 %reduce-scatter.7.cloned.1.call-done = bf16[256,128]{1,0:T(8,128)(2,1)} async-done(((bf16[1024,128]{1,0:T(8,128)(2,1)}), bf16[256,128]{1,0:T(8,128)(2,1)}) %reduce-scatter.7.cloned.1.call-update) | async-done | bytes 65552 | tf_op jit(solution)/shard_map/reduce_scatter | solution.py:39
  205.0 31.8 %all_gather.14 = bf16[2048,128]{1,0:T(8,128)(2,1)S(1)} all-gather(bf16[256,128]{1,0:T(8,128)(2,1)S(1)} %fusion.57), channel_id=1, replica_groups=mesh['row'=8,'col'=4] {'row'}, dimensions={0}, use_global_device_ids=true | all-gather | bytes 589824 | tf_op jit(solution)/shard_map/all_gather | solution.py:25
  236.8 12.2 %gather_fusion.2 = bf16[160,128,128]{2,1,0:T(8,128)(2,1)} fusion(bf16[8,2,128,128]{3,2,1,0:T(8,128)(2,1)S(1)} %bitcast.96, s32[160]{0:T(256)S(1)} %reshape.99), kind=kCustom, calls=%fused_computation.2.clone | custom fusion | bytes 10487040 | tf_op jit(solution)/shard_map/jit(take_along_axis)/gather | solution.py:28
  248.9 10.0 %fusion.10 = f32[8,20,128,128]{3,2,1,0:T(8,128)} fusion(bf16[1,1,8,20,128,128]{5,4,3,2,1,0:T(8,128)(2,1)} %param.11, bf16[8,20,128,128]{3,2,1,0:T(8,128)(2,1)} %bitcast.101, pred[8,20]{1,0:T(8,128)(4,1)S(1)} %and_bitcast_fusion), kind=kOutput, calls=%fused_computation.14 | convolution fusion | flops 673710080 | bytes 20971680 | tf_op jit(solution)/shard_map/qtkn,qtks->qtns/dot_general | solution.py:29
  258.9 11.9 %copy.15 = f32[8,20,128,128]{2,1,0,3:T(8,128)} copy(f32[8,20,128,128]{3,2,1,0:T(8,128)} %fusion.10) | data formatting | bytes 20971520 | tf_op jit(solution)/shard_map/qtkn,qtks->qtns/dot_general | solution.py:29
  279.7 20.1 %reduce-scatter.9.cloned.1.call-done = bf16[256,128]{1,0:T(8,128)(2,1)} async-done(((bf16[1024,128]{1,0:T(8,128)(2,1)}), bf16[256,128]{1,0:T(8,128)(2,1)}) %reduce-scatter.9.cloned.1.call-update) | async-done | bytes 65552 | tf_op jit(solution)/shard_map/reduce_scatter | solution.py:39
  301.6 31.7 %all_gather.15 = bf16[2048,128]{1,0:T(8,128)(2,1)S(1)} all-gather(bf16[256,128]{1,0:T(8,128)(2,1)S(1)} %fusion.60), channel_id=1, replica_groups=mesh['row'=8,'col'=4] {'row'}, dimensions={0}, use_global_device_ids=true | all-gather | bytes 589824 | tf_op jit(solution)/shard_map/all_gather | solution.py:25
  333.3 12.2 %gather_fusion.3 = bf16[160,128,128]{2,1,0:T(8,128)(2,1)} fusion(bf16[8,2,128,128]{3,2,1,0:T(8,128)(2,1)S(1)} %bitcast.94, s32[160]{0:T(256)S(1)} %reshape.99), kind=kCustom, calls=%fused_computation.3.clone | custom fusion | bytes 10487040 | tf_op jit(solution)/shard_map/jit(take_along_axis)/gather | solution.py:28
  345.4 10.0 %fusion.8 = f32[8,20,128,128]{3,2,1,0:T(8,128)} fusion(bf16[1,1,8,20,128,128]{5,4,3,2,1,0:T(8,128)(2,1)} %param.11, bf16[8,20,128,128]{3,2,1,0:T(8,128)(2,1)} %bitcast.98, pred[8,20]{1,0:T(8,128)(4,1)S(1)} %and_bitcast_fusion), kind=kOutput, calls=%fused_computation.12 | convolution fusion | flops 673710080 | bytes 20971680 | tf_op jit(solution)/shard_map/qtkn,qtks->qtns/dot_general | solution.py:29
  355.5 11.9 %copy.17 = f32[8,20,128,128]{2,1,0,3:T(8,128)} copy(f32[8,20,128,128]{3,2,1,0:T(8,128)} %fusion.8) | data formatting | bytes 20971520 | tf_op jit(solution)/shard_map/qtkn,qtks->qtns/dot_general | solution.py:29
  367.4 8.1 %fusion.40 = bf16[8,128,128]{2,0,1:T(8,128)(2,1)S(1)} fusion(f32[8,20,128,128]{2,1,0,3:T(8,128)} %copy.17, s32[8,20]{1,0:T(8,128)S(1)} %bitcast.109), kind=kOutput, calls=%fused_computation.36 | convolution fusion | flops 251790592 | bytes 10748544 | tf_op jit(solution)/shard_map/qtm,qtns->mns/dot_general | solution.py:32
  376.3 20.2 %reduce-scatter.11.cloned.1.call-done = bf16[256,128]{1,0:T(8,128)(2,1)} async-done(((bf16[1024,128]{1,0:T(8,128)(2,1)}), bf16[256,128]{1,0:T(8,128)(2,1)}) %reduce-scatter.11.cloned.1.call-update) | async-done | bytes 65552 | tf_op jit(solution)/shard_map/reduce_scatter | solution.py:39
  398.2 39.3 %all-reduce = (f32[128]{0:T(128)S(1)}, f32[128]{0:T(128)S(1)}, f32[128]{0:T(128)S(1)}, f32[128]{0:T(128)S(1)}, f32[128]{0:T(128)S(1)}, /*index=5*/f32[128]{0:T(128)S(1)}, f32[128]{0:T(128)S(1)}, f32[128]{0:T(128)S(1)}) all-reduce(f32[128]{0:T(128)S(1)} %get-tuple-element.10, ...), channel_id=1, replica_groups=mesh['row'=8,'col'=4] {'row','col'}, use_global_device_ids=true, to_apply=%region_5.7 | all-reduce | flops 1024 | bytes 8192 | tf_op jit(solution)/shard_map/psum | solution.py:49
  (40 shorter events, 21.4 us)
Async XLA Ops:
  7.2 99.1 %reduce-scatter.5.cloned.1.call-start = ((), (), s32[]{:S(2)}) async-start(), calls=%async_computation.4 | async-start | bytes 327680 | tf_op jit(solution)/shard_map/reduce_scatter | solution.py:39
  64.1 11.9 %copy-start.5 = (s32[1,1,8,20]{3,2,1,0:T(8,128)S(1)}, s32[1,1,8,20]{3,2,1,0:T(8,128)}, u32[]{:S(2)}) copy-start(s32[1,1,8,20]{3,2,1,0:T(8,128)} %param.10) | copy-start | bytes 1924
  76.0 30.2 %copy-start = (bf16[256,128]{1,0:T(8,128)(2,1)S(1)}, bf16[256,128]{1,0:T(8,128)(2,1)}, u32[]{:S(2)}) copy-start(bf16[256,128]{1,0:T(8,128)(2,1)} %param.7) | copy-start | bytes 196612
  76.0 30.2 %copy-start.4 = (s32[256,128]{1,0:T(8,128)S(1)}, s32[256,128]{1,0:T(8,128)}, u32[]{:S(2)}) copy-start(s32[256,128]{1,0:T(8,128)} %param.8) | copy-start | bytes 393220
  85.0 118.2 %reduce-scatter.7.cloned.1.call-start = ((), (), s32[]{:S(2)}) async-start(), calls=%async_computation.5 | async-start | bytes 327680 | tf_op jit(solution)/shard_map/reduce_scatter | solution.py:39
  183.1 116.7 %reduce-scatter.9.cloned.1.call-start = ((), (), s32[]{:S(2)}) async-start(), calls=%async_computation.6 | async-start | bytes 327680 | tf_op jit(solution)/shard_map/reduce_scatter | solution.py:39
  279.7 116.8 %reduce-scatter.11.cloned.1.call-start = ((), (), s32[]{:S(2)}) async-start(), calls=%async_computation.7 | async-start | bytes 327680 | tf_op jit(solution)/shard_map/reduce_scatter | solution.py:39
  367.4 70.2 %copy-start.1 = (bf16[256,128]{1,0:T(8,128)(2,1)S(1)}, bf16[256,128]{1,0:T(8,128)(2,1)}, u32[]{:S(2)}) copy-start(bf16[256,128]{1,0:T(8,128)(2,1)} %reduce-scatter.5.cloned.1.call-done) | copy-start | bytes 196612
  367.4 70.2 %copy-start.2 = (bf16[256,128]{1,0:T(8,128)(2,1)S(1)}, bf16[256,128]{1,0:T(8,128)(2,1)}, u32[]{:S(2)}) copy-start(bf16[256,128]{1,0:T(8,128)(2,1)} %reduce-scatter.9.cloned.1.call-done) | copy-start | bytes 196612
  367.4 70.2 %copy-start.3 = (bf16[256,128]{1,0:T(8,128)(2,1)S(1)}, bf16[256,128]{1,0:T(8,128)(2,1)}, u32[]{:S(2)}) copy-start(bf16[256,128]{1,0:T(8,128)(2,1)} %reduce-scatter.7.cloned.1.call-done) | copy-start | bytes 196612
Sparse Core Ops, SparseCore 0:
  85.1 21.0 reduce-scatter.4
  183.2 19.9 reduce-scatter.6
  279.8 19.9 reduce-scatter.8
  376.4 20.0 reduce-scatter.10
where the time goes:
time: 455 us; the launch traced here: 446 us
  blocking collectives  168 us (37%)
  local copies, waits for them, and re-layouts  99.3 us (22%)
  waiting for transfers between devices  81.6 us (18%)
  matrix products  72.5 us (16%)
  between operations  14.1 us (3%)
  other arithmetic  10.1 us (2%)
    all_gather x4, blocking collectives, on_device(): gathered = lax.all_gather(current, 'row', axis=0, tiled=True)  129 us
    reduce_scatter x4, waiting for transfers between devices, on_device(): lax.psum_scatter(partial_value.reshape(-1, sources).astype(jnp.bfloat16),...  81.6 us
    gather x5, local copies, waits for them, and re-layouts, on_device(): picked = jnp.take_along_axis(blocked, row_index[:, :, None, None], axis=1)  48.7 us
    dot_general x4, local copies, waits for them, and re-layouts, on_device(): jnp.einsum('qtkn,qtks->qtns', tile_data, picked, preferred_element_type=j...  47.7 us
    dot_general x4, matrix products, on_device(): jnp.einsum('qtkn,qtks->qtns', tile_data, picked, preferred_element_type=j...  40.1 us
    psum x1, blocking collectives, on_device(): counted, totals = lax.psum((counted, totals), ('row', 'col'))  39.3 us
    dot_general x4, matrix products, on_device(): jnp.einsum('qtm,qtns->mns', col_onehot, products, precision=lax.Precision...  32.4 us
  transfers between devices with their start and end apart: 4, of which 4 were waited for; matrix products, arithmetic and copies ran while one was open for 0% of the time, Pallas kernels for 0%

commit v1 on v0

--- a/solution.py
+++ b/solution.py
@@ -46,7 +46,7 @@
         reached = jnp.where(newly_hit, raw_sum, jnp.zeros_like(raw_sum))
         counted = jnp.sum(newly_hit.astype(jnp.float32), axis=0)
         totals = jnp.sum(reached, axis=0)
-        counted, totals = lax.psum((counted, totals), ("row", "col"))
+        counted, totals = lax.psum(lax.psum((counted, totals), "col"), "row")
         scaling = scaling / jnp.maximum(scaling * totals / jnp.maximum(counted, 1.0), 1.0)
         reach_out = reach_out + scaling[None, :] * reached
         depth_out = jnp.where(newly_hit, level_step, depth_out)

time: 455 us -> 443 us (0.974)
  blocking collectives: 168 us -> 156 us
    psum x1 -> x2, blocking collectives: 39.3 us -> 27.3 us  [on_device(): counted, totals = lax.psum(lax.psum((counted, totals), 'col'), 'row')]
where the time goes in v1:
time: 443 us; the launch traced here: 434 us
  blocking collectives  156 us (35%)
  local copies, waits for them, and re-layouts  99.3 us (22%)
  waiting for transfers between devices  81.6 us (18%)
  matrix products  72.5 us (16%)
  between operations  14.1 us (3%)
  other arithmetic  10.1 us (2%)
    all_gather x4, blocking collectives, on_device(): gathered = lax.all_gather(current, 'row', axis=0, tiled=True)  129 us
    reduce_scatter x4, waiting for transfers between devices, on_device(): lax.psum_scatter(partial_value.reshape(-1, sources).astype(jnp.bfloat16),...  81.6 us
    gather x5, local copies, waits for them, and re-layouts, on_device(): picked = jnp.take_along_axis(blocked, row_index[:, :, None, None], axis=1)  48.7 us
    dot_general x4, local copies, waits for them, and re-layouts, on_device(): jnp.einsum('qtkn,qtks->qtns', tile_data, picked, preferred_element_type=j...  47.7 us
    dot_general x4, matrix products, on_device(): jnp.einsum('qtkn,qtks->qtns', tile_data, picked, preferred_element_type=j...  40.1 us
    dot_general x4, matrix products, on_device(): jnp.einsum('qtm,qtns->mns', col_onehot, products, precision=lax.Precision...  32.4 us
    psum x2, blocking collectives, on_device(): counted, totals = lax.psum(lax.psum((counted, totals), 'col'), 'row')  27.3 us
  transfers between devices with their start and end apart: 4, of which 4 were waited for; matrix products, arithmetic and copies ran while one was open for 0% of the time, Pallas kernels for 0%

profile of v1, /device:TPU:0, one launch (start us, length us, event | category | flops | bytes accessed | tf_op | source)
XLA Modules:
  0.0 433.9 jit_solution(12744772902998167258)
XLA Ops:
  8.7 33.2 %all_gather.12 = bf16[2048,128]{1,0:T(8,128)(2,1)S(1)} all-gather(bf16[256,128]{1,0:T(8,128)(2,1)} %param.7), channel_id=1, replica_groups=mesh['row'=8,'col'=4] {'row'}, dimensions={0}, use_global_device_ids=true | all-gather | bytes 589824 | tf_op jit(solution)/shard_map/all_gather | solution.py:25
  41.9 12.2 %gather_fusion = bf16[160,128,128]{2,1,0:T(8,128)(2,1)} fusion(bf16[8,2,128,128]{3,2,1,0:T(8,128)(2,1)S(1)} %bitcast.97, s32[160]{0:T(256)S(1)} %reshape.99), kind=kCustom, calls=%fused_computation.clone | custom fusion | bytes 10487040 | tf_op jit(solution)/shard_map/jit(take_along_axis)/gather | solution.py:28
  54.1 10.0 %fusion.14 = f32[8,20,128,128]{3,2,1,0:T(8,128)} fusion(bf16[1,1,8,20,128,128]{5,4,3,2,1,0:T(8,128)(2,1)} %param.11, bf16[8,20,128,128]{3,2,1,0:T(8,128)(2,1)} %bitcast.99, pred[8,20]{1,0:T(8,128)(4,1)S(1)} %and_bitcast_fusion), kind=kOutput, calls=%fused_computation.18 | convolution fusion | flops 673710080 | bytes 20971680 | tf_op jit(solution)/shard_map/qtkn,qtks->qtns/dot_general | solution.py:29
  64.1 11.9 %copy.11 = f32[8,20,128,128]{2,1,0,3:T(8,128)} copy(f32[8,20,128,128]{3,2,1,0:T(8,128)} %fusion.14) | data formatting | bytes 20971520 | tf_op jit(solution)/shard_map/qtkn,qtks->qtns/dot_general | solution.py:29
  76.0 8.2 %fusion.49 = bf16[8,128,128]{2,0,1:T(8,128)(2,1)S(1)} fusion(f32[8,20,128,128]{2,1,0,3:T(8,128)} %copy.11, s32[8,20]{1,0:T(8,128)S(1)} %bitcast.106), kind=kOutput, calls=%fused_computation.39 | convolution fusion | flops 251790592 | bytes 10748544 | tf_op jit(solution)/shard_map/qtm,qtns->mns/dot_general | solution.py:32
  85.0 21.2 %reduce-scatter.5.cloned.1.call-done = bf16[256,128]{1,0:T(8,128)(2,1)} async-done(((bf16[1024,128]{1,0:T(8,128)(2,1)}), bf16[256,128]{1,0:T(8,128)(2,1)}) %reduce-scatter.5.cloned.1.call-update) | async-done | bytes 65552 | tf_op jit(solution)/shard_map/reduce_scatter | solution.py:39
  108.0 32.1 %all_gather.13 = bf16[2048,128]{1,0:T(8,128)(2,1)S(1)} all-gather(bf16[256,128]{1,0:T(8,128)(2,1)S(1)} %fusion.54), channel_id=1, replica_groups=mesh['row'=8,'col'=4] {'row'}, dimensions={0}, use_global_device_ids=true | all-gather | bytes 589824 | tf_op jit(solution)/shard_map/all_gather | solution.py:25
  140.1 12.2 %gather_fusion.1 = bf16[160,128,128]{2,1,0:T(8,128)(2,1)} fusion(bf16[8,2,128,128]{3,2,1,0:T(8,128)(2,1)S(1)} %bitcast.95, s32[160]{0:T(256)S(1)} %reshape.99), kind=kCustom, calls=%fused_computation.1.clone | custom fusion | bytes 10487040 | tf_op jit(solution)/shard_map/jit(take_along_axis)/gather | solution.py:28
  152.3 10.0 %fusion.12 = f32[8,20,128,128]{3,2,1,0:T(8,128)} fusion(bf16[1,1,8,20,128,128]{5,4,3,2,1,0:T(8,128)(2,1)} %param.11, bf16[8,20,128,128]{3,2,1,0:T(8,128)(2,1)} %bitcast.100, pred[8,20]{1,0:T(8,128)(4,1)S(1)} %and_bitcast_fusion), kind=kOutput, calls=%fused_computation.16 | convolution fusion | flops 673710080 | bytes 20971680 | tf_op jit(solution)/shard_map/qtkn,qtks->qtns/dot_general | solution.py:29
  162.3 11.9 %copy.13 = f32[8,20,128,128]{2,1,0,3:T(8,128)} copy(f32[8,20,128,128]{3,2,1,0:T(8,128)} %fusion.12) | data formatting | bytes 20971520 | tf_op jit(solution)/shard_map/qtkn,qtks->qtns/dot_general | solution.py:29
  174.2 8.1 %fusion.46 = bf16[8,128,128]{2,0,1:T(8,128)(2,1)S(1)} fusion(f32[8,20,128,128]{2,1,0,3:T(8,128)} %copy.13, s32[8,20]{1,0:T(8,128)S(1)} %bitcast.107), kind=kOutput, calls=%fused_computation.38 | convolution fusion | flops 251790592 | bytes 10748544 | tf_op jit(solution)/shard_map/qtm,qtns->mns/dot_general | solution.py:32
  183.1 20.1 %reduce-scatter.7.cloned.1.call-done = bf16[256,128]{1,0:T(8,128)(2,1)} async-done(((bf16[1024,128]{1,0:T(8,128)(2,1)}), bf16[256,128]{1,0:T(8,128)(2,1)}) %reduce-scatter.7.cloned.1.call-update) | async-done | bytes 65552 | tf_op jit(solution)/shard_map/reduce_scatter | solution.py:39
  205.0 31.8 %all_gather.14 = bf16[2048,128]{1,0:T(8,128)(2,1)S(1)} all-gather(bf16[256,128]{1,0:T(8,128)(2,1)S(1)} %fusion.57), channel_id=1, replica_groups=mesh['row'=8,'col'=4] {'row'}, dimensions={0}, use_global_device_ids=true | all-gather | bytes 589824 | tf_op jit(solution)/shard_map/all_gather | solution.py:25
  236.8 12.2 %gather_fusion.2 = bf16[160,128,128]{2,1,0:T(8,128)(2,1)} fusion(bf16[8,2,128,128]{3,2,1,0:T(8,128)(2,1)S(1)} %bitcast.96, s32[160]{0:T(256)S(1)} %reshape.99), kind=kCustom, calls=%fused_computation.2.clone | custom fusion | bytes 10487040 | tf_op jit(solution)/shard_map/jit(take_along_axis)/gather | solution.py:28
  248.9 10.0 %fusion.10 = f32[8,20,128,128]{3,2,1,0:T(8,128)} fusion(bf16[1,1,8,20,128,128]{5,4,3,2,1,0:T(8,128)(2,1)} %param.11, bf16[8,20,128,128]{3,2,1,0:T(8,128)(2,1)} %bitcast.101, pred[8,20]{1,0:T(8,128)(4,1)S(1)} %and_bitcast_fusion), kind=kOutput, calls=%fused_computation.14 | convolution fusion | flops 673710080 | bytes 20971680 | tf_op jit(solution)/shard_map/qtkn,qtks->qtns/dot_general | solution.py:29
  258.9 11.9 %copy.15 = f32[8,20,128,128]{2,1,0,3:T(8,128)} copy(f32[8,20,128,128]{3,2,1,0:T(8,128)} %fusion.10) | data formatting | bytes 20971520 | tf_op jit(solution)/shard_map/qtkn,qtks->qtns/dot_general | solution.py:29
  279.7 20.1 %reduce-scatter.9.cloned.1.call-done = bf16[256,128]{1,0:T(8,128)(2,1)} async-done(((bf16[1024,128]{1,0:T(8,128)(2,1)}), bf16[256,128]{1,0:T(8,128)(2,1)}) %reduce-scatter.9.cloned.1.call-update) | async-done | bytes 65552 | tf_op jit(solution)/shard_map/reduce_scatter | solution.py:39
  301.6 31.7 %all_gather.15 = bf16[2048,128]{1,0:T(8,128)(2,1)S(1)} all-gather(bf16[256,128]{1,0:T(8,128)(2,1)S(1)} %fusion.60), channel_id=1, replica_groups=mesh['row'=8,'col'=4] {'row'}, dimensions={0}, use_global_device_ids=true | all-gather | bytes 589824 | tf_op jit(solution)/shard_map/all_gather | solution.py:25
  333.3 12.2 %gather_fusion.3 = bf16[160,128,128]{2,1,0:T(8,128)(2,1)} fusion(bf16[8,2,128,128]{3,2,1,0:T(8,128)(2,1)S(1)} %bitcast.94, s32[160]{0:T(256)S(1)} %reshape.99), kind=kCustom, calls=%fused_computation.3.clone | custom fusion | bytes 10487040 | tf_op jit(solution)/shard_map/jit(take_along_axis)/gather | solution.py:28
  345.4 10.0 %fusion.8 = f32[8,20,128,128]{3,2,1,0:T(8,128)} fusion(bf16[1,1,8,20,128,128]{5,4,3,2,1,0:T(8,128)(2,1)} %param.11, bf16[8,20,128,128]{3,2,1,0:T(8,128)(2,1)} %bitcast.98, pred[8,20]{1,0:T(8,128)(4,1)S(1)} %and_bitcast_fusion), kind=kOutput, calls=%fused_computation.12 | convolution fusion | flops 673710080 | bytes 20971680 | tf_op jit(solution)/shard_map/qtkn,qtks->qtns/dot_general | solution.py:29
  355.5 11.9 %copy.17 = f32[8,20,128,128]{2,1,0,3:T(8,128)} copy(f32[8,20,128,128]{3,2,1,0:T(8,128)} %fusion.8) | data formatting | bytes 20971520 | tf_op jit(solution)/shard_map/qtkn,qtks->qtns/dot_general | solution.py:29
  367.4 8.1 %fusion.40 = bf16[8,128,128]{2,0,1:T(8,128)(2,1)S(1)} fusion(f32[8,20,128,128]{2,1,0,3:T(8,128)} %copy.17, s32[8,20]{1,0:T(8,128)S(1)} %bitcast.109), kind=kOutput, calls=%fused_computation.36 | convolution fusion | flops 251790592 | bytes 10748544 | tf_op jit(solution)/shard_map/qtm,qtns->mns/dot_general | solution.py:32
  376.3 20.2 %reduce-scatter.11.cloned.1.call-done = bf16[256,128]{1,0:T(8,128)(2,1)} async-done(((bf16[1024,128]{1,0:T(8,128)(2,1)}), bf16[256,128]{1,0:T(8,128)(2,1)}) %reduce-scatter.11.cloned.1.call-update) | async-done | bytes 65552 | tf_op jit(solution)/shard_map/reduce_scatter | solution.py:39
  403.9 21.6 %all-reduce = (f32[128]{0:T(128)S(1)}, f32[128]{0:T(128)S(1)}, f32[128]{0:T(128)S(1)}, f32[128]{0:T(128)S(1)}, f32[128]{0:T(128)S(1)}, /*index=5*/f32[128]{0:T(128)S(1)}, f32[128]{0:T(128)S(1)}, f32[128]{0:T(128)S(1)}) all-reduce(f32[128]{0:T(128)S(1)} %get-tuple-element.19, ...), channel_id=1, replica_groups=mesh['row'=8,'col'=4] {'row'}, use_global_device_ids=true, to_apply=%region_6.8 | all-reduce | flops 1024 | bytes 8192 | tf_op jit(solution)/shard_map/psum | solution.py:49
  (41 shorter events, 27.2 us)
Async XLA Ops:
  7.2 99.1 %reduce-scatter.5.cloned.1.call-start = ((), (), s32[]{:S(2)}) async-start(), calls=%async_computation.4 | async-start | bytes 327680 | tf_op jit(solution)/shard_map/reduce_scatter | solution.py:39
  64.1 11.9 %copy-start.5 = (s32[1,1,8,20]{3,2,1,0:T(8,128)S(1)}, s32[1,1,8,20]{3,2,1,0:T(8,128)}, u32[]{:S(2)}) copy-start(s32[1,1,8,20]{3,2,1,0:T(8,128)} %param.10) | copy-start | bytes 1924
  76.0 30.2 %copy-start = (bf16[256,128]{1,0:T(8,128)(2,1)S(1)}, bf16[256,128]{1,0:T(8,128)(2,1)}, u32[]{:S(2)}) copy-start(bf16[256,128]{1,0:T(8,128)(2,1)} %param.7) | copy-start | bytes 196612
  76.0 30.2 %copy-start.4 = (s32[256,128]{1,0:T(8,128)S(1)}, s32[256,128]{1,0:T(8,128)}, u32[]{:S(2)}) copy-start(s32[256,128]{1,0:T(8,128)} %param.8) | copy-start | bytes 393220
  85.0 118.2 %reduce-scatter.7.cloned.1.call-start = ((), (), s32[]{:S(2)}) async-start(), calls=%async_computation.5 | async-start | bytes 327680 | tf_op jit(solution)/shard_map/reduce_scatter | solution.py:39
  183.1 116.7 %reduce-scatter.9.cloned.1.call-start = ((), (), s32[]{:S(2)}) async-start(), calls=%async_computation.6 | async-start | bytes 327680 | tf_op jit(solution)/shard_map/reduce_scatter | solution.py:39
  279.7 116.8 %reduce-scatter.11.cloned.1.call-start = ((), (), s32[]{:S(2)}) async-start(), calls=%async_computation.7 | async-start | bytes 327680 | tf_op jit(solution)/shard_map/reduce_scatter | solution.py:39
  367.4 58.1 %copy-start.1 = (bf16[256,128]{1,0:T(8,128)(2,1)S(1)}, bf16[256,128]{1,0:T(8,128)(2,1)}, u32[]{:S(2)}) copy-start(bf16[256,128]{1,0:T(8,128)(2,1)} %reduce-scatter.5.cloned.1.call-done) | copy-start | bytes 196612
  367.4 58.1 %copy-start.2 = (bf16[256,128]{1,0:T(8,128)(2,1)S(1)}, bf16[256,128]{1,0:T(8,128)(2,1)}, u32[]{:S(2)}) copy-start(bf16[256,128]{1,0:T(8,128)(2,1)} %reduce-scatter.9.cloned.1.call-done) | copy-start | bytes 196612
  367.4 58.2 %copy-start.3 = (bf16[256,128]{1,0:T(8,128)(2,1)S(1)}, bf16[256,128]{1,0:T(8,128)(2,1)}, u32[]{:S(2)}) copy-start(bf16[256,128]{1,0:T(8,128)(2,1)} %reduce-scatter.7.cloned.1.call-done) | copy-start | bytes 196612
Sparse Core Ops, SparseCore 0:
  85.1 21.0 reduce-scatter.4
  183.2 19.9 reduce-scatter.6
  279.8 19.9 reduce-scatter.8
  376.4 20.0 reduce-scatter.10
